TPU v7x, 32 devices: a whole 2x2x4 slice. The times are simulated.
32 devices in a mesh: clip: 4 (over x, core), seq: 2 (over y), head: 4 (over z).
Axes of the slice: x: 2, y: 2, z: 4, core: 2. Of those that a mesh axis runs over, the one named last changes fastest.
Arguments:
- inputs: bfloat16 [4, 1500, 768], P('clip', 'seq'), may hold values from -6 to 6
- gain_one: bfloat16 [768], P(('clip', 'seq')), may hold values from 0.25 to 1.75
- shift_one: bfloat16 [768], P(('clip', 'seq')), may hold values from -1.75 to 1.75
- w_query: bfloat16 [768, 768], P(('clip', 'seq'), 'head'), may hold values from -0.21875 to 0.21875
- b_query: bfloat16 [768], P('head'), may hold values from -3 to 3
- w_key: bfloat16 [768, 768], P(('clip', 'seq'), 'head'), may hold values from -0.21875 to 0.21875
- w_value: bfloat16 [768, 768], P(('clip', 'seq'), 'head'), may hold values from -0.21875 to 0.21875
- b_value: bfloat16 [768], P('head'), may hold values from -0.3125 to 0.3125
- w_out: bfloat16 [768, 768], P('head', ('clip', 'seq')), may hold values from -3.5 to 3.5
- b_out: bfloat16 [768], P(('clip', 'seq')), may hold values from -3 to 3
- gain_two: bfloat16 [768], P(('clip', 'seq')), may hold values from 0.25 to 1.75
- shift_two: bfloat16 [768], P(('clip', 'seq')), may hold values from -1.75 to 1.75
- w_fc_one: bfloat16 [768, 3072], P(('clip', 'seq'), 'head'), may hold values from -0.21875 to 0.21875
- b_fc_one: bfloat16 [3072], P('head'), may hold values from -3 to 3
- w_fc_two: bfloat16 [3072, 768], P('head', ('clip', 'seq')), may hold values from -0.3125 to 0.3125
- b_fc_two: bfloat16 [768], P(('clip', 'seq')), may hold values from -3 to 3
- cotangent: bfloat16 [4, 1500, 768], P('clip', 'seq'), may hold values from -6 to 6
Outputs:
- outputs: bfloat16 [4, 1500, 768], P('clip', 'seq')
- input_gradient: float32 [4, 1500, 768], P('clip', 'seq')
- first_gain_gradient: float32 [768], P(('clip', 'seq'))
- grad_shift_one: float32 [768], P(('clip', 'seq'))
- grad_w_query: float32 [768, 768], P(('clip', 'seq'), 'head')
- grad_b_query: float32 [768], P('head')
- grad_w_key: float32 [768, 768], P(('clip', 'seq'), 'head')
- grad_w_value: float32 [768, 768], P(('clip', 'seq'), 'head')
- grad_b_value: float32 [768], P('head')
- grad_w_out: float32 [768, 768], P('head', ('clip', 'seq'))
- grad_b_out: float32 [768], P(('clip', 'seq'))
- second_gain_gradient: float32 [768], P(('clip', 'seq'))
- grad_shift_two: float32 [768], P(('clip', 'seq'))
- grad_w_fc_one: float32 [768, 3072], P(('clip', 'seq'), 'head')
- grad_b_fc_one: float32 [3072], P('head')
- grad_w_fc_two: float32 [3072, 768], P('head', ('clip', 'seq'))
- grad_b_fc_two: float32 [768], P(('clip', 'seq'))
All inputs are finite; a program needn't handle non-finite values.
Results may differ from a plain program's by a relative error of at most 0.012.
Values may be sent and summed in bfloat16 or wider, within the bound.
A program may use at most 128 MiB of HBM per device.

v0:
```python
from functools import partial
import jax
import jax.numpy as jnp
from jax import lax
from jax.sharding import PartitionSpec as P

HEAD_DIM = 64
eps = 1e-05


def layer_norm_forward(values, norm_gain, norm_shift):
    row_mean = jnp.mean(values, axis=-1, keepdims=True)
    centered_values = values - row_mean
    spread = jnp.mean(centered_values * centered_values, axis=-1, keepdims=True)
    inverse_deviation = lax.rsqrt(spread + eps)
    standardized = centered_values * inverse_deviation
    return (standardized * norm_gain + norm_shift, standardized, inverse_deviation)


def layer_norm_backward(output_gradient, standardized, inverse_deviation, norm_gain):
    scaled_rows = output_gradient * norm_gain
    first_row_mean = jnp.mean(scaled_rows, axis=-1, keepdims=True)
    second_row_mean = jnp.mean(scaled_rows * standardized, axis=-1, keepdims=True)
    return inverse_deviation * (scaled_rows - first_row_mean - standardized * second_row_mean)


def fetch_weights(
    gain_one,
    shift_one,
    w_query,
    w_key,
    w_value,
    b_out,
    gain_two,
    shift_two,
    w_fc_one,
    b_fc_two,
    w_out,
    w_fc_two,
):
    rows = (
        lax.all_gather(gain_one, ("clip", "seq"), axis=0, tiled=True),
        lax.all_gather(shift_one, ("clip", "seq"), axis=0, tiled=True),
        lax.all_gather(w_query, ("clip", "seq"), axis=0, tiled=True),
        lax.all_gather(w_key, ("clip", "seq"), axis=0, tiled=True),
        lax.all_gather(w_value, ("clip", "seq"), axis=0, tiled=True),
        lax.all_gather(b_out, ("clip", "seq"), axis=0, tiled=True),
        lax.all_gather(gain_two, ("clip", "seq"), axis=0, tiled=True),
        lax.all_gather(shift_two, ("clip", "seq"), axis=0, tiled=True),
        lax.all_gather(w_fc_one, ("clip", "seq"), axis=0, tiled=True),
        lax.all_gather(b_fc_two, ("clip", "seq"), axis=0, tiled=True),
    )
    columns = (
        lax.all_gather(w_out, ("clip", "seq"), axis=1, tiled=True),
        lax.all_gather(w_fc_two, ("clip", "seq"), axis=1, tiled=True),
    )
    return (rows, columns)


def head_total(partial_sum):
    return lax.psum(partial_sum, "head")


def on_device(
    inputs,
    gain_one,
    shift_one,
    w_query,
    b_query,
    w_key,
    w_value,
    b_value,
    w_out,
    b_out,
    gain_two,
    shift_two,
    w_fc_one,
    b_fc_one,
    w_fc_two,
    b_fc_two,
    cotangent,
):
    clips, frames, width = inputs.shape
    local = w_query.shape[1]
    heads = local // HEAD_DIM
    scale = HEAD_DIM ** (-0.5)
    gathered_rows = jnp.float32
    count = clips * frames
    rows, columns = fetch_weights(
        gain_one,
        shift_one,
        w_query,
        w_key,
        w_value,
        b_out,
        gain_two,
        shift_two,
        w_fc_one,
        b_fc_two,
        w_out,
        w_fc_two,
    )
    (
        full_gain_one,
        gathered_first_shift,
        full_query,
        full_key,
        full_value,
        full_b_out,
        full_gain_two,
        gathered_second_shift,
        full_fc_one,
        full_b_fc_two,
    ) = rows
    full_out, full_fc_two = columns
    token_rows = inputs.astype(gathered_rows).reshape(count, width)
    first_norm_gain = full_gain_one.astype(gathered_rows)
    second_norm_gain = full_gain_two.astype(gathered_rows)
    normalized_gathered, first_standardized, first_inverse_deviation = layer_norm_forward(
        token_rows, first_norm_gain, gathered_first_shift.astype(gathered_rows)
    )
    normed_one = normalized_gathered.astype(jnp.bfloat16)
    query = (
        jnp.dot(normed_one, full_query, preferred_element_type=gathered_rows)
        + b_query.astype(gathered_rows)
    ).astype(jnp.bfloat16)
    key = jnp.dot(normed_one, full_key, preferred_element_type=gathered_rows).astype(jnp.bfloat16)
    value = (
        jnp.dot(normed_one, full_value, preferred_element_type=gathered_rows)
        + b_value.astype(gathered_rows)
    ).astype(jnp.bfloat16)
    query_clips = query.reshape(clips, frames, local)
    key_all, value_all = (
        lax.all_gather(key.reshape(clips, frames, local), "seq", axis=1, tiled=True),
        lax.all_gather(value.reshape(clips, frames, local), "seq", axis=1, tiled=True),
    )

    def attend(block):
        query_block, key_block, value_block = block
        query_heads = query_block.reshape(frames, heads, HEAD_DIM)
        key_heads = key_block.reshape(-1, heads, HEAD_DIM)
        value_heads = value_block.reshape(-1, heads, HEAD_DIM)
        scores = (
            jnp.einsum("qhd,khd->hqk", query_heads, key_heads, preferred_element_type=gathered_rows)
            * scale
        )
        top = jnp.max(scores, axis=-1, keepdims=True)
        expo = jnp.exp(scores - top)
        total = jnp.sum(expo, axis=-1, keepdims=True)
        probs = (expo / total).astype(jnp.bfloat16)
        result = jnp.einsum(
            "hqk,khd->qhd", probs, value_heads, preferred_element_type=gathered_rows
        )
        return (result.reshape(frames, local).astype(jnp.bfloat16), (top + jnp.log(total))[..., 0])

    attended_clips, log_totals = lax.map(attend, (query_clips, key_all, value_all))
    attended = attended_clips.reshape(count, local)
    attn_terms = jnp.dot(attended, full_out, preferred_element_type=gathered_rows)
    middle_state = token_rows + head_total(attn_terms) + full_b_out.astype(gathered_rows)
    normalized_middle, second_standardized, second_inverse_deviation = layer_norm_forward(
        middle_state, second_norm_gain, gathered_second_shift.astype(gathered_rows)
    )
    normed_two = normalized_middle.astype(jnp.bfloat16)
    pre = jnp.dot(normed_two, full_fc_one, preferred_element_type=gathered_rows) + b_fc_one.astype(
        gathered_rows
    )
    act = jax.nn.gelu(pre, approximate=False).astype(jnp.bfloat16)
    ffn_terms = jnp.dot(act, full_fc_two, preferred_element_type=gathered_rows)
    outputs = (middle_state + head_total(ffn_terms) + full_b_fc_two.astype(gathered_rows)).astype(
        jnp.bfloat16
    )
    rows, columns = fetch_weights(
        gain_one,
        shift_one,
        w_query,
        w_key,
        w_value,
        b_out,
        gain_two,
        shift_two,
        w_fc_one,
        b_fc_two,
        w_out,
        w_fc_two,
    )
    (
        full_gain_one,
        gathered_first_shift,
        full_query,
        full_key,
        full_value,
        full_b_out,
        full_gain_two,
        gathered_second_shift,
        full_fc_one,
        full_b_fc_two,
    ) = rows
    full_out, full_fc_two = columns
    first_norm_gain = full_gain_one.astype(gathered_rows)
    second_norm_gain = full_gain_two.astype(gathered_rows)
    upstream_gradient = cotangent.astype(gathered_rows).reshape(count, width)
    grad_b_fc_two = jnp.sum(upstream_gradient, axis=0)
    grad_top_low = upstream_gradient.astype(jnp.bfloat16)
    grad_w_fc_two = jnp.einsum("tf,td->fd", act, grad_top_low, preferred_element_type=gathered_rows)
    grad_act = jnp.einsum(
        "td,fd->tf", grad_top_low, full_fc_two, preferred_element_type=gathered_rows
    )
    unused, gelu_back = jax.vjp(partial(jax.nn.gelu, approximate=False), pre)
    grad_pre = gelu_back(grad_act)[0].astype(jnp.bfloat16)
    grad_b_fc_one = jnp.sum(grad_pre.astype(gathered_rows), axis=0)
    grad_w_fc_one = jnp.einsum(
        "td,tf->df", normed_two, grad_pre, preferred_element_type=gathered_rows
    )
    normed_two_terms = jnp.einsum(
        "tf,df->td", grad_pre, full_fc_one, preferred_element_type=gathered_rows
    )
    second_normalized_gradient = head_total(normed_two_terms)
    middle_gradient = upstream_gradient + layer_norm_backward(
        second_normalized_gradient, second_standardized, second_inverse_deviation, second_norm_gain
    )
    grad_mid_low = middle_gradient.astype(jnp.bfloat16)
    second_gain_gradient = jnp.sum(second_normalized_gradient * second_standardized, axis=0)
    grad_shift_two = jnp.sum(second_normalized_gradient, axis=0)
    grad_b_out = jnp.sum(middle_gradient, axis=0)
    grad_w_out = jnp.einsum(
        "tj,td->jd", attended, grad_mid_low, preferred_element_type=gathered_rows
    )
    grad_attended = jnp.einsum(
        "td,jd->tj", grad_mid_low, full_out, preferred_element_type=gathered_rows
    ).astype(jnp.bfloat16)

    def attend_back(block):
        query_block, key_block, value_block, grad_block, log_block = block
        query_heads = query_block.reshape(frames, heads, HEAD_DIM)
        key_heads = key_block.reshape(-1, heads, HEAD_DIM)
        value_heads = value_block.reshape(-1, heads, HEAD_DIM)
        grad_heads = grad_block.reshape(frames, heads, HEAD_DIM)
        scores = (
            jnp.einsum("qhd,khd->hqk", query_heads, key_heads, preferred_element_type=gathered_rows)
            * scale
        )
        probs = jnp.exp(scores - log_block[..., None])
        grad_values = jnp.einsum(
            "hqk,qhd->khd",
            probs.astype(jnp.bfloat16),
            grad_heads,
            preferred_element_type=gathered_rows,
        )
        grad_probs = jnp.einsum(
            "qhd,khd->hqk", grad_heads, value_heads, preferred_element_type=gathered_rows
        )
        inner = jnp.sum(probs * grad_probs, axis=-1, keepdims=True)
        grad_scores = (probs * (grad_probs - inner)).astype(jnp.bfloat16)
        grad_queries = (
            jnp.einsum("hqk,khd->qhd", grad_scores, key_heads, preferred_element_type=gathered_rows)
            * scale
        )
        grad_keys = (
            jnp.einsum(
                "hqk,qhd->khd", grad_scores, query_heads, preferred_element_type=gathered_rows
            )
            * scale
        )
        return (
            grad_queries.reshape(frames, local).astype(jnp.bfloat16),
            grad_keys.reshape(-1, local),
            grad_values.reshape(-1, local),
        )

    grad_query_clips, grad_key_all, grad_value_all = lax.map(
        attend_back,
        (query_clips, key_all, value_all, grad_attended.reshape(clips, frames, local), log_totals),
    )
    grad_key_own, grad_value_own = (
        lax.psum_scatter(grad_key_all, "seq", scatter_dimension=1, tiled=True),
        lax.psum_scatter(grad_value_all, "seq", scatter_dimension=1, tiled=True),
    )
    grad_query = grad_query_clips.reshape(count, local)
    grad_key = grad_key_own.reshape(count, local).astype(jnp.bfloat16)
    grad_value = grad_value_own.reshape(count, local).astype(jnp.bfloat16)
    grad_b_query = jnp.sum(grad_query.astype(gathered_rows), axis=0)
    grad_b_value = jnp.sum(grad_value.astype(gathered_rows), axis=0)
    grad_w_query = jnp.einsum(
        "td,tj->dj", normed_one, grad_query, preferred_element_type=gathered_rows
    )
    grad_w_key = jnp.einsum("td,tj->dj", normed_one, grad_key, preferred_element_type=gathered_rows)
    grad_w_value = jnp.einsum(
        "td,tj->dj", normed_one, grad_value, preferred_element_type=gathered_rows
    )
    grad_normed_part = jnp.einsum(
        "tj,dj->td", grad_query, full_query, preferred_element_type=gathered_rows
    )
    grad_normed_part = grad_normed_part + jnp.einsum(
        "tj,dj->td", grad_key, full_key, preferred_element_type=gathered_rows
    )
    grad_normed_part = grad_normed_part + jnp.einsum(
        "tj,dj->td", grad_value, full_value, preferred_element_type=gathered_rows
    )
    first_normalized_gradient = head_total(grad_normed_part)
    first_gain_gradient = jnp.sum(first_normalized_gradient * first_standardized, axis=0)
    grad_shift_one = jnp.sum(first_normalized_gradient, axis=0)
    input_gradient = middle_gradient + layer_norm_backward(
        first_normalized_gradient, first_standardized, first_inverse_deviation, first_norm_gain
    )
    owned_rows = (
        lax.psum_scatter(first_gain_gradient, ("clip", "seq"), scatter_dimension=0, tiled=True),
        lax.psum_scatter(grad_shift_one, ("clip", "seq"), scatter_dimension=0, tiled=True),
        lax.psum_scatter(grad_w_query, ("clip", "seq"), scatter_dimension=0, tiled=True),
        lax.psum_scatter(grad_w_key, ("clip", "seq"), scatter_dimension=0, tiled=True),
        lax.psum_scatter(grad_w_value, ("clip", "seq"), scatter_dimension=0, tiled=True),
        lax.psum_scatter(grad_b_out, ("clip", "seq"), scatter_dimension=0, tiled=True),
        lax.psum_scatter(second_gain_gradient, ("clip", "seq"), scatter_dimension=0, tiled=True),
        lax.psum_scatter(grad_shift_two, ("clip", "seq"), scatter_dimension=0, tiled=True),
        lax.psum_scatter(grad_w_fc_one, ("clip", "seq"), scatter_dimension=0, tiled=True),
        lax.psum_scatter(grad_b_fc_two, ("clip", "seq"), scatter_dimension=0, tiled=True),
    )
    owned_columns = (
        lax.psum_scatter(grad_w_out, ("clip", "seq"), scatter_dimension=1, tiled=True),
        lax.psum_scatter(grad_w_fc_two, ("clip", "seq"), scatter_dimension=1, tiled=True),
    )
    bias_totals = lax.psum((grad_b_query, grad_b_value, grad_b_fc_one), ("clip", "seq"))
    return (
        outputs.reshape(clips, frames, width),
        input_gradient.reshape(clips, frames, width),
        owned_rows[0],
        owned_rows[1],
        owned_rows[2],
        bias_totals[0],
        owned_rows[3],
        owned_rows[4],
        bias_totals[1],
        owned_columns[0],
        owned_rows[5],
        owned_rows[6],
        owned_rows[7],
        owned_rows[8],
        bias_totals[2],
        owned_columns[1],
        owned_rows[9],
    )


def solution(mesh):
    return jax.shard_map(
        on_device,
        mesh=mesh,
        in_specs=(
            P("clip", "seq", None),
            P(("clip", "seq")),
            P(("clip", "seq")),
            P(("clip", "seq"), "head"),
            P("head"),
            P(("clip", "seq"), "head"),
            P(("clip", "seq"), "head"),
            P("head"),
            P("head", ("clip", "seq")),
            P(("clip", "seq")),
            P(("clip", "seq")),
            P(("clip", "seq")),
            P(("clip", "seq"), "head"),
            P("head"),
            P("head", ("clip", "seq")),
            P(("clip", "seq")),
            P("clip", "seq", None),
        ),
        out_specs=(
            P("clip", "seq", None),
            P("clip", "seq", None),
            P(("clip", "seq")),
            P(("clip", "seq")),
            P(("clip", "seq"), "head"),
            P("head"),
            P(("clip", "seq"), "head"),
            P(("clip", "seq"), "head"),
            P("head"),
            P("head", ("clip", "seq")),
            P(("clip", "seq")),
            P(("clip", "seq")),
            P(("clip", "seq")),
            P(("clip", "seq"), "head"),
            P("head"),
            P("head", ("clip", "seq")),
            P(("clip", "seq")),
        ),
        check_vma=False,
    )
```

profile of v0, /device:TPU:0, one launch (start us, length us, event | category | flops | bytes accessed | tf_op | source)
XLA Modules:
  0.0 687.4 jit_solution(10025798544051608802)
XLA Ops:
  15.1 25.7 %all-reduce.17 = (bf16[768]{0:T(1024)(128)(2,1)S(1)}, bf16[768]{0:T(1024)(128)(2,1)S(1)}, bf16[768]{0:T(1024)(128)(2,1)S(1)}, bf16[768]{0:T(1024)(128)(2,1)S(1)}...) all-reduce(bf16[768]{0:T(1024)(128)(2,1)S(1)} %dynamic-update-slice, ...), channel_id=1, replica_groups=mesh['clip'=4,'seq'=2,'head'=4] {'clip','seq'}, use_global_device_ids=true, to_apply=%add.1 | all-reduce | flops 4608 | bytes 18432
  44.1 15.9 %all_gather.55 = bf16[768,192]{1,0:T(8,128)(2,1)S(1)} all-gather(bf16[96,192]{1,0:T(8,128)(2,1)S(1)} %copy-done.26), channel_id=1, replica_groups=mesh['clip'=4,'seq'=2,'head'=4] {'clip','seq'}, dimensions={0}, use_global_device_ids=true | all-gather | bytes 331776 | tf_op jit(solution)/shard_map/all_gather | solution.py:45
  61.1 10.5 %all-gather.3 = bf16[2,750,192]{1,2,0:T(8,128)(2,1)S(1)} all-gather(bf16[1,750,192]{1,2,0:T(8,128)(2,1)S(1)} %fusion.39), channel_id=3, replica_groups=mesh['clip'=4,'seq'=2,'head'=4] {'seq'}, dimensions={0}, use_global_device_ids=true | all-gather | bytes 864000 | tf_op jit(solution)/shard_map/all_gather | solution.py:134
  75.3 15.6 %all_gather.54 = bf16[768,192]{1,0:T(8,128)(2,1)S(1)} all-gather(bf16[96,192]{1,0:T(8,128)(2,1)S(1)} %copy-done.27), channel_id=1, replica_groups=mesh['clip'=4,'seq'=2,'head'=4] {'clip','seq'}, dimensions={0}, use_global_device_ids=true | all-gather | bytes 331776 | tf_op jit(solution)/shard_map/all_gather | solution.py:44
  91.0 16.6 %all_gather.52 = bf16[768,192]{1,0:T(8,128)(2,1)S(1)} all-gather(bf16[96,192]{1,0:T(8,128)(2,1)S(1)} %copy-done.28), channel_id=1, replica_groups=mesh['clip'=4,'seq'=2,'head'=4] {'clip','seq'}, dimensions={0}, use_global_device_ids=true | all-gather | bytes 331776 | tf_op jit(solution)/shard_map/all_gather | solution.py:46
  108.9 9.9 %all-gather.2 = bf16[2,750,192]{1,2,0:T(8,128)(2,1)S(1)} all-gather(bf16[1,750,192]{1,2,0:T(8,128)(2,1)S(1)} %fusion.40), channel_id=2, replica_groups=mesh['clip'=4,'seq'=2,'head'=4] {'seq'}, dimensions={0}, use_global_device_ids=true | all-gather | bytes 864000 | tf_op jit(solution)/shard_map/all_gather | solution.py:135
  123.2 16.6 %all_gather.57 = bf16[192,768]{0,1:T(8,128)(2,1)S(1)} all-gather(bf16[192,96]{0,1:T(8,128)(2,1)S(1)} %copy.40), channel_id=1, replica_groups=mesh['clip'=4,'seq'=2,'head'=4] {'clip','seq'}, dimensions={1}, use_global_device_ids=true | all-gather | bytes 331776 | tf_op jit(solution)/shard_map/all_gather | solution.py:54
  140.4 7.0 %multiply_reduce_fusion.1 = (f32[3,750]{1,0:T(4,128)S(1)}, f32[3,750,1500]{2,1,0:T(8,128)}) fusion(bf16[750,3,64]{0,2,1:T(8,128)(2,1)S(1)} %bitcast.146, bf16[1500,3,64]{0,2,1:T(8,128)(2,1)S(1)} %reshape.253), kind=kOutput, calls=%fused_computation.6 | convolution fusion | flops 438747744 | bytes 14373000 | tf_op jit(solution)/shard_map/while/body/eval_jaxpr/qhd,khd->hqk/dot_general | solution.py:144
  147.4 7.4 %fusion = f32[3,750]{1,0:T(4,128)S(1)} fusion(f32[3,750,1500]{2,1,0:T(8,128)} %get-tuple-element.151, f32[3,750]{1,0:T(4,128)S(1)} %get-tuple-element.150), kind=kLoop, calls=%fused_computation.5 | loop fusion | flops 10122750 | bytes 13518000 | tf_op jit(solution)/shard_map/while/body/eval_jaxpr/reduce_sum | solution.py:149
  154.8 6.6 fusion.38
  164.7 94.1 %all-reduce.23.cloned.1.call-done = f32[750,768]{1,0:T(8,128)} async-done(((f32[750,768]{1,0:T(8,128)}), f32[750,768]{1,0:T(8,128)}) %all-reduce.23.cloned.1.call-update) | async-done | bytes 2304016 | tf_op jit(solution)/shard_map/psum | solution.py:61
  261.2 8.9 %multiply_convert_fusion.1 = (bf16[750,768]{1,0:T(8,128)(2,1)}, f32[750,768]{1,0:T(8,128)}, f32[750,768]{1,0:T(8,128)}) fusion(f32[768]{0:T(1024)S(1)} %convert_element_type.151, bf16[768,768]{1,0:T(8,128)(2,1)} %all-gather.7.cloned.1.call-done, f32[750,768]{1,0:T(8,128)S(1)} %get-tuple-element.147, f32[768]{0:T(1024)S(1)} %convert_element_type.149, ...), kind=kOutput, calls=%fused_computation.48 | convolution fusion | flops 925632000 | bytes 9258864 | tf_op jit(solution)/shard_map/dot_general | solution.py:164
  270.1 4.8 convert_reduce_fusion.2
  280.3 4.1 fusion.71
  284.4 86.5 %all-reduce.25.cloned.1.call-done = f32[750,768]{1,0:T(8,128)} async-done(((f32[750,768]{1,0:T(8,128)}), f32[750,768]{1,0:T(8,128)}) %all-reduce.25.cloned.1.call-update) | async-done | bytes 2304016 | tf_op jit(solution)/shard_map/psum | solution.py:61
  376.9 7.7 %fusion.2 = f32[3,64,1500]{2,1,0:T(8,128)} fusion(bf16[750,3,64]{0,2,1:T(8,128)(2,1)S(1)} %bitcast.144, f32[3,750,1500]{2,1,0:T(8,128)} %get-tuple-element.151, f32[3,750]{1,0:T(4,128)S(1)} %log_add_fusion), kind=kOutput, calls=%fused_computation.8 | convolution fusion | flops 442124992 | bytes 14949000 | tf_op jit(solution)/shard_map/while/body/eval_jaxpr/hqk,qhd->khd/dot_general | solution.py:243
  384.6 7.0 %multiply_reduce_fusion = (f32[3,750]{1,0:T(4,128)S(1)}, f32[3,750,1500]{2,1,0:T(8,128)}) fusion(f32[3,750,1500]{2,1,0:T(8,128)S(1)} %bitcast.141, f32[3,750]{1,0:T(4,128)S(1)} %log_add_fusion, bf16[750,3,64]{0,2,1:T(8,128)(2,1)S(1)} %bitcast.145, bf16[1500,3,64]{0,2,1:T(8,128)(2,1)S(1)} %copy-done.18), kind=kOutput, calls=%fused_computation.1 | convolution fusion | flops 445497760 | bytes 27882000 | tf_op jit(solution)/shard_map/while/body/eval_jaxpr/qhd,khd->hqk/dot_general | solution.py:249
  391.6 6.9 multiply_convert_fusion
  405.2 62.3 %all-reduce.28 = (bf16[1,1500,192]{1,2,0:T(8,128)(2,1)}, bf16[1,1500,192]{1,2,0:T(8,128)(2,1)}) all-reduce(f32[1,1500,192]{1,2,0:T(8,128)} %bitcast.142, f32[1,1500,192]{1,2,0:T(8,128)} %bitcast.143), channel_id=4, replica_groups=mesh['clip'=4,'seq'=2,'head'=4] {'seq'}, use_global_device_ids=true, to_apply=%region_12.13.clone | all-reduce | flops 576000 | bytes 3456000
  481.9 4.2 fusion.61
  486.1 4.2 fusion.43
  494.2 145.7 %all-reduce.27.cloned.1.call-done = (f32[750,768]{1,0:T(8,128)}, f32[750,768]{1,0:T(8,128)}) async-done(((f32[750,768]{1,0:T(8,128)}, f32[750,768]{1,0:T(8,128)}), (f32[750,768]{1,0:T(8,128)}, f32[750,768]{1,0:T(8,128)})) %all-reduce.27.cloned.1.call-update) | async-done | bytes 4608016 | tf_op jit(solution)/shard_map/psum | solution.py:61
  642.5 25.1 %all-reduce.14 = (f32[768]{0:T(1024)S(1)}, f32[768]{0:T(1024)S(1)}, f32[192]{0:T(256)}, f32[192]{0:T(256)}, f32[768]{0:T(1024)S(1)}, /*index=5*/f32[768]{0:T(102...) all-reduce(f32[768]{0:T(1024)S(1)} %get-tuple-element.115, ...), channel_id=6, replica_groups=mesh['clip'=4,'seq'=2,'head'=4] {'clip','seq'}, use_global_device_ids=true, to_apply=%region_18.19.clone | all-reduce | flops 5760 | bytes 46080
  673.9 3.8 copy.41
  (183 shorter events, 72.3 us)
Async XLA Ops:
  8.0 52.0 %copy-start = (bf16[1,750,768]{2,1,0:T(8,128)(2,1)S(1)}, bf16[1,750,768]{2,1,0:T(8,128)(2,1)}, u32[]{:S(2)}) copy-start(bf16[1,750,768]{2,1,0:T(8,128)(2,1)} %param.17) | copy-start | bytes 3456004
  8.0 36.0 %copy-start.26 = (bf16[96,192]{1,0:T(8,128)(2,1)S(1)}, bf16[96,192]{1,0:T(8,128)(2,1)}, u32[]{:S(2)}) copy-start(bf16[96,192]{1,0:T(8,128)(2,1)} %param.22) | copy-start | bytes 110596
  8.0 250.7 %all-reduce.23.cloned.1.call-start = ((), (), s32[]{:S(2)}) async-start(), calls=%async_computation.6 | async-start | bytes 4620288 | tf_op jit(solution)/shard_map/psum | solution.py:61
  60.0 11.6 %copy-start.8 = (bf16[768,192]{1,0:T(8,128)(2,1)}, bf16[768,192]{1,0:T(8,128)(2,1)S(1)}, u32[]{:S(2)}) copy-start(bf16[768,192]{1,0:T(8,128)(2,1)S(1)} %all_gather.55) | copy-start | bytes 884740
  60.5 14.8 %copy-start.27 = (bf16[96,192]{1,0:T(8,128)(2,1)S(1)}, bf16[96,192]{1,0:T(8,128)(2,1)}, u32[]{:S(2)}) copy-start(bf16[96,192]{1,0:T(8,128)(2,1)} %param.20) | copy-start | bytes 110596
  60.5 30.5 %copy-start.32 = (bf16[192]{0:T(256)(128)(2,1)S(1)}, bf16[192]{0:T(256)(128)(2,1)}, u32[]{:S(2)}) copy-start(bf16[192]{0:T(256)(128)(2,1)} %param.21) | copy-start | bytes 1156
  60.5 30.5 %copy-start.28 = (bf16[96,192]{1,0:T(8,128)(2,1)S(1)}, bf16[96,192]{1,0:T(8,128)(2,1)}, u32[]{:S(2)}) copy-start(bf16[96,192]{1,0:T(8,128)(2,1)} %param.23) | copy-start | bytes 110596
  61.1 46.5 %copy-start.33 = (bf16[192]{0:T(256)(128)(2,1)S(1)}, bf16[192]{0:T(256)(128)(2,1)}, u32[]{:S(2)}) copy-start(bf16[192]{0:T(256)(128)(2,1)} %param.24) | copy-start | bytes 1156
  75.3 65.1 %copy-start.5 = (bf16[1500,3,64]{0,2,1:T(8,128)(2,1)}, bf16[1500,3,64]{0,2,1:T(8,128)(2,1)S(1)}, u32[]{:S(2)}) copy-start(bf16[1500,3,64]{0,2,1:T(8,128)(2,1)S(1)} %reshape.253) | copy-start | bytes 1728004
  91.0 48.8 %copy-start.9 = (bf16[768,192]{1,0:T(8,128)(2,1)}, bf16[768,192]{1,0:T(8,128)(2,1)S(1)}, u32[]{:S(2)}) copy-start(bf16[768,192]{1,0:T(8,128)(2,1)S(1)} %all_gather.54) | copy-start | bytes 884740
  108.4 14.7 %copy-start.29 = (bf16[192,96]{1,0:T(8,128)(2,1)S(1)}, bf16[192,96]{1,0:T(8,128)(2,1)}, u32[]{:S(2)}) copy-start(bf16[192,96]{1,0:T(8,128)(2,1)} %param.25) | copy-start | bytes 110596
  139.8 21.6 %copy-start.11 = (bf16[192,768]{0,1:T(8,128)(2,1)}, bf16[192,768]{0,1:T(8,128)(2,1)S(1)}, u32[]{:S(2)}) copy-start(bf16[192,768]{0,1:T(8,128)(2,1)S(1)} %all_gather.57) | copy-start | bytes 884740
  163.4 97.8 %all-gather.7.cloned.1.call-start = ((), (), s32[]{:S(2)}) async-start(), calls=%async_computation.7 | async-start | bytes 1327104 | tf_op jit(solution)/shard_map/all_gather | solution.py:50
  164.0 106.1 %all-gather.9.cloned.1.call-start = ((), (), s32[]{:S(2)}) async-start(), calls=%async_computation.8 | async-start | bytes 1327104 | tf_op jit(solution)/shard_map/all_gather | solution.py:55
  164.6 206.4 %all-reduce.25.cloned.1.call-start = ((), (), s32[]{:S(2)}) async-start(), calls=%async_computation.9 | async-start | bytes 4620288 | tf_op jit(solution)/shard_map/psum | solution.py:61
  278.4 214.1 %reduce-scatter.21.cloned.1.call-start = ((), (), s32[]{:S(2)}) async-start(), calls=%async_computation.15 | async-start | bytes 884736
  373.8 10.8 %slice-start = ((s8[13860864]{0:T(1024)(128)(4,1)}), s8[4194304]{0:T(1024)(128)(4,1)S(1)}, s32[]{:S(2)}) async-start(s8[13860864]{0:T(1024)(128)(4,1)} %bitcast.140), calls=%async_computation.17 | async-start | bytes 8388608
  373.8 10.8 %slice-start.1 = ((s8[13860864]{0:T(1024)(128)(4,1)}), s8[4194304]{0:T(1024)(128)(4,1)S(1)}, s32[]{:S(2)}) async-start(s8[13860864]{0:T(1024)(128)(4,1)} %bitcast.140), calls=%async_computation.18 | async-start | bytes 8388608
  405.2 234.7 %all-reduce.27.cloned.1.call-start = ((), (), s32[]{:S(2)}) async-start(), calls=%async_computation.16 | async-start | bytes 9240576 | tf_op jit(solution)/shard_map/psum | solution.py:61
  472.4 206.7 %reduce-scatter.15.cloned.1.call-start = ((), (), s32[]{:S(2)}) async-start(), calls=%async_computation.12 | async-start | bytes 884736 | tf_op jit(solution)/shard_map/reduce_scatter | solution.py:310
  475.6 203.5 %reduce-scatter.13.cloned.1.call-start = ((), (), s32[]{:S(2)}) async-start(), calls=%async_computation.11 | async-start | bytes 884736 | tf_op jit(solution)/shard_map/reduce_scatter | solution.py:309
  479.0 200.0 %reduce-scatter.11.cloned.1.call-start = ((), (), s32[]{:S(2)}) async-start(), calls=%async_computation.10 | async-start | bytes 884736 | tf_op jit(solution)/shard_map/reduce_scatter | solution.py:308
  481.8 197.3 %reduce-scatter.17.cloned.1.call-start = ((), (), s32[]{:S(2)}) async-start(), calls=%async_computation.13 | async-start | bytes 2654208 | tf_op jit(solution)/shard_map/reduce_scatter | solution.py:314
  486.1 194.0 %reduce-scatter.19.cloned.1.call-start = ((), (), s32[]{:S(2)}) async-start(), calls=%async_computation.14 | async-start | bytes 2654208 | tf_op jit(solution)/shard_map/reduce_scatter | solution.py:319
  (27 other events, 92.8 us)
Sparse Core Ops, SparseCore 0:
  163.5 95.1 all-reduce.22
  278.5 92.3 all-reduce.24
  472.5 167.2 all-reduce.26
Sparse Core Ops, SparseCore 1:
  165.8 25.6 all-gather.6
  193.2 23.8 all-gather.8
  405.3 36.4 reduce-scatter.20
  476.9 33.4 reduce-scatter.14
  514.1 34.9 reduce-scatter.12
  552.8 34.9 reduce-scatter.10
  591.5 42.2 reduce-scatter.16
  637.6 42.4 reduce-scatter.18
where the time goes:
time: 695 us; the launch traced here: 687 us
  waiting for transfers between devices  328 us (47%)
  blocking collectives  198 us (28%)
  matrix products  79.4 us (11%)
  other arithmetic  33.5 us (5%)
  local copies, waits for them, and re-layouts  28.8 us (4%)
  between operations  18.1 us (3%)
    psum x3, waiting for transfers between devices, head_total(): return lax.psum(partial_sum, 'head')  326 us
    unnamed x3, blocking collectives  113 us
    unnamed x103, local copies, waits for them, and re-layouts  20.8 us
    all_gather x1, blocking collectives, fetch_weights(): lax.all_gather(w_value, ('clip', 'seq'), axis=0, tiled=True)  16.6 us
    all_gather x1, blocking collectives, fetch_weights(): lax.all_gather(w_out, ('clip', 'seq'), axis=1, tiled=True)  16.6 us
    all_gather x1, blocking collectives, fetch_weights(): lax.all_gather(w_key, ('clip', 'seq'), axis=0, tiled=True)  15.9 us
    all_gather x1, blocking collectives, fetch_weights(): lax.all_gather(w_query, ('clip', 'seq'), axis=0, tiled=True)  15.6 us
  transfers between devices with their start and end apart: 11, of which 4 were waited for; matrix products, arithmetic and copies ran while one was open for 8% of the time, Pallas kernels for 0%

commit v1 on v0

--- a/solution.py
+++ b/solution.py
@@ -58,7 +58,7 @@
 
 
 def head_total(partial_sum):
-    return lax.psum(partial_sum, "head")
+    return jnp.sum(lax.all_gather(partial_sum, "head"), axis=0)
 
 
 def on_device(

time: 695 us -> 1140 us (1.64)
  waiting for transfers between devices: 328 us -> 742 us
  other arithmetic: 33.5 us -> 65.2 us
    all_gather x0 -> x4, waiting for transfers between devices: none -> 515 us  [head_total(): return jnp.sum(lax.all_gather(partial_sum, 'head'), axis=0)]
    psum x3 -> x0, waiting for transfers between devices: 326 us -> none  [head_total(): return lax.psum(partial_sum, 'head')]
    reduce_scatter x1, waiting for transfers between devices: 0.97 us -> 46.3 us  [on_device(): lax.psum_scatter(grad_w_fc_two, ('clip', 'seq'), scatter_dimension=1, til...]
    reduce_scatter x1, waiting for transfers between devices: 0.01 us -> 38.7 us  [on_device(): lax.psum_scatter(grad_w_query, ('clip', 'seq'), scatter_dimension=0, tile...]
    reduce_scatter x1, waiting for transfers between devices: 0.01 us -> 38.5 us  [on_device(): lax.psum_scatter(grad_w_value, ('clip', 'seq'), scatter_dimension=0, tile...]
    reduce_scatter x1, waiting for transfers between devices: 0.01 us -> 38.5 us  [on_device(): lax.psum_scatter(grad_w_key, ('clip', 'seq'), scatter_dimension=0, tiled=...]
    reduce_sum x1 -> x4, other arithmetic: 1.48 us -> 22 us  [the longest x2 11.8 us: head_total(): return jnp.sum(lax.all_gather(partial_sum, 'head'), axis=0)]
    all_gather x1, waiting for transfers between devices: 0.01 us -> 16.9 us  [fetch_weights(): lax.all_gather(w_fc_two, ('clip', 'seq'), axis=1, tiled=True)]
  transfers between devices with their start and end apart: 11 -> 12, of which waited for: 4 -> 12; matrix products, arithmetic and copies ran while one was open for 8% -> 10% of each run, Pallas kernels for 0% -> 0%
where the time goes in v1:
time: 1140 us; the launch traced here: 1130 us
  waiting for transfers between devices  742 us (65%)
  blocking collectives  200 us (18%)
  matrix products  80.8 us (7%)
  other arithmetic  65.2 us (6%)
  local copies, waits for them, and re-layouts  28.3 us (2%)
  between operations  16.9 us (1%)
    all_gather x4, waiting for transfers between devices, head_total(): return jnp.sum(lax.all_gather(partial_sum, 'head'), axis=0)  515 us
    unnamed x3, blocking collectives  110 us
    reduce_scatter x1, waiting for transfers between devices, on_device(): lax.psum_scatter(grad_w_fc_two, ('clip', 'seq'), scatter_dimension=1, til...  46.3 us
    reduce_scatter x1, waiting for transfers between devices, on_device(): lax.psum_scatter(grad_w_query, ('clip', 'seq'), scatter_dimension=0, tile...  38.7 us
    reduce_scatter x1, waiting for transfers between devices, on_device(): lax.psum_scatter(grad_w_value, ('clip', 'seq'), scatter_dimension=0, tile...  38.5 us
    reduce_scatter x1, waiting for transfers between devices, on_device(): lax.psum_scatter(grad_w_key, ('clip', 'seq'), scatter_dimension=0, tiled=...  38.5 us
  transfers between devices with their start and end apart: 12, of which 12 were waited for; matrix products, arithmetic and copies ran while one was open for 10% of the time, Pallas kernels for 0%

profile of v1, /device:TPU:0, one launch (start us, length us, event | category | flops | bytes accessed | tf_op | source)
XLA Modules:
  0.0 1134.1 jit_solution(9684092934496129819)
XLA Ops:
  15.7 25.7 %all-reduce.16 = (bf16[768]{0:T(1024)(128)(2,1)S(1)}, bf16[768]{0:T(1024)(128)(2,1)S(1)}, bf16[768]{0:T(1024)(128)(2,1)S(1)}, bf16[768]{0:T(1024)(128)(2,1)S(1)}...) all-reduce(bf16[768]{0:T(1024)(128)(2,1)S(1)} %dynamic-update-slice, ...), channel_id=1, replica_groups=mesh['clip'=4,'seq'=2,'head'=4] {'clip','seq'}, use_global_device_ids=true, to_apply=%add.1 | all-reduce | flops 4608 | bytes 18432
  44.8 15.9 %all_gather.81 = bf16[192,768]{0,1:T(8,128)(2,1)S(1)} all-gather(bf16[192,96]{0,1:T(8,128)(2,1)S(1)} %copy.42), channel_id=1, replica_groups=mesh['clip'=4,'seq'=2,'head'=4] {'clip','seq'}, dimensions={1}, use_global_device_ids=true | all-gather | bytes 331776 | tf_op jit(solution)/shard_map/all_gather | solution.py:54
  60.7 19.2 %all_gather.78 = bf16[768,192]{1,0:T(8,128)(2,1)} all-gather(bf16[96,192]{1,0:T(8,128)(2,1)S(1)} %copy-done.26), channel_id=1, replica_groups=mesh['clip'=4,'seq'=2,'head'=4] {'clip','seq'}, dimensions={0}, use_global_device_ids=true | all-gather | bytes 331776 | tf_op jit(solution)/shard_map/all_gather | solution.py:44
  79.9 15.9 %all_gather.79 = bf16[768,192]{1,0:T(8,128)(2,1)S(1)} all-gather(bf16[96,192]{1,0:T(8,128)(2,1)S(1)} %copy-done.27), channel_id=1, replica_groups=mesh['clip'=4,'seq'=2,'head'=4] {'clip','seq'}, dimensions={0}, use_global_device_ids=true | all-gather | bytes 331776 | tf_op jit(solution)/shard_map/all_gather | solution.py:45
  95.7 19.2 %all_gather.76 = bf16[768,192]{1,0:T(8,128)(2,1)} all-gather(bf16[96,192]{1,0:T(8,128)(2,1)S(1)} %copy-done.28), channel_id=1, replica_groups=mesh['clip'=4,'seq'=2,'head'=4] {'clip','seq'}, dimensions={0}, use_global_device_ids=true | all-gather | bytes 331776 | tf_op jit(solution)/shard_map/all_gather | solution.py:46
  116.0 10.0 all-gather.7
  131.4 9.4 all-gather.6
  172.4 161.8 %all-gather.23.cloned.1.call-done = f32[4,750,768]{2,1,0:T(8,128)} async-done(((f32[1,750,768]{2,1,0:T(8,128)}), f32[4,750,768]{2,1,0:T(8,128)}) %all-gather.23.cloned.1.call-update) | async-done | bytes 9216016 | tf_op jit(solution)/shard_map/all_gather | solution.py:61
  342.6 15.6 %all-gather.19.cloned.1.call-done = bf16[768,768]{1,0:T(8,128)(2,1)} async-done(((bf16[96,768]{1,0:T(8,128)(2,1)}), bf16[768,768]{1,0:T(8,128)(2,1)}) %all-gather.19.cloned.1.call-update) | async-done | bytes 1179664 | tf_op jit(solution)/shard_map/all_gather | solution.py:50
  358.2 8.9 multiply_convert_fusion.1
  367.1 16.9 %all-gather.21.cloned.1.call-done = bf16[768,768]{0,1:T(8,128)(2,1)} async-done(((bf16[768,96]{0,1:T(8,128)(2,1)}), bf16[768,768]{0,1:T(8,128)(2,1)}) %all-gather.21.cloned.1.call-update) | async-done | bytes 1179664 | tf_op jit(solution)/shard_map/all_gather | solution.py:55
  398.4 157.6 %all-gather.27.cloned.1.call-done = f32[4,750,768]{2,1,0:T(8,128)} async-done(((f32[1,750,768]{2,1,0:T(8,128)}), f32[4,750,768]{2,1,0:T(8,128)}) %all-gather.27.cloned.1.call-update) | async-done | bytes 9216016 | tf_op jit(solution)/shard_map/all_gather | solution.py:61
  565.2 8.7 fusion.2
  591.3 60.2 %all-reduce.18 = (bf16[1,1500,192]{1,2,0:T(8,128)(2,1)}, bf16[1,1500,192]{1,2,0:T(8,128)(2,1)}) all-reduce(f32[1,1500,192]{1,2,0:T(8,128)} %bitcast.164, f32[1,1500,192]{1,2,0:T(8,128)} %bitcast.165), channel_id=8, replica_groups=mesh['clip'=4,'seq'=2,'head'=4] {'seq'}, use_global_device_ids=true, to_apply=%region_12.13.clone | all-reduce | flops 576000 | bytes 3456000
  663.2 55.9 %all-gather.25.cloned.1.call-done = f32[4,750,768]{2,1,0:T(8,128)} async-done(((f32[1,750,768]{2,1,0:T(8,128)}), f32[4,750,768]{2,1,0:T(8,128)}) %all-gather.25.cloned.1.call-update) | async-done | bytes 9216016 | tf_op jit(solution)/shard_map/all_gather | solution.py:61
  743.1 139.3 %all-gather.29.cloned.1.call-done = f32[4,750,768]{2,1,0:T(8,128)} async-done(((f32[1,750,768]{2,1,0:T(8,128)}), f32[4,750,768]{2,1,0:T(8,128)}) %all-gather.29.cloned.1.call-update) | async-done | bytes 9216016 | tf_op jit(solution)/shard_map/all_gather | solution.py:61
  889.1 10.0 add_convert_fusion.2
  904.4 14.2 %reduce-scatter.21.cloned.1.call-done = f32[96,192]{1,0:T(8,128)} async-done(((f32[768,192]{1,0:T(8,128)}), f32[96,192]{1,0:T(8,128)}) %reduce-scatter.21.cloned.1.call-update) | async-done | bytes 73744
  920.3 24.4 %all-reduce.14 = (f32[768]{0:T(1024)S(1)}, f32[768]{0:T(1024)S(1)}, f32[192]{0:T(256)}, f32[192]{0:T(256)}, f32[768]{0:T(1024)S(1)}, /*index=5*/f32[768]{0:T(102...) all-reduce(f32[768]{0:T(1024)S(1)} %get-tuple-element.68, ...), channel_id=10, replica_groups=mesh['clip'=4,'seq'=2,'head'=4] {'clip','seq'}, use_global_device_ids=true, to_apply=%region_18.19.clone | all-reduce | flops 5760 | bytes 46080
  948.2 16.8 %reduce-scatter.17.cloned.1.call-done = f32[96,768]{1,0:T(8,128)} async-done(((f32[768,768]{1,0:T(8,128)}), f32[96,768]{1,0:T(8,128)}) %reduce-scatter.17.cloned.1.call-update) | async-done | bytes 294928 | tf_op jit(solution)/shard_map/reduce_scatter | solution.py:314
  965.0 46.3 %reduce-scatter.19.cloned.1.call-done = f32[768,96]{0,1:T(8,128)} async-done(((f32[768,768]{0,1:T(8,128)}), f32[768,96]{0,1:T(8,128)}) %reduce-scatter.19.cloned.1.call-update) | async-done | bytes 294928 | tf_op jit(solution)/shard_map/reduce_scatter | solution.py:319
  1011.3 38.5 %reduce-scatter.13.cloned.1.call-done = f32[96,192]{1,0:T(8,128)} async-done(((f32[768,192]{1,0:T(8,128)}), f32[96,192]{1,0:T(8,128)}) %reduce-scatter.13.cloned.1.call-update) | async-done | bytes 73744 | tf_op jit(solution)/shard_map/reduce_scatter | solution.py:309
  1049.8 38.7 %reduce-scatter.11.cloned.1.call-done = f32[96,192]{1,0:T(8,128)} async-done(((f32[768,192]{1,0:T(8,128)}), f32[96,192]{1,0:T(8,128)}) %reduce-scatter.11.cloned.1.call-update) | async-done | bytes 73744 | tf_op jit(solution)/shard_map/reduce_scatter | solution.py:308
  1088.5 38.5 %reduce-scatter.15.cloned.1.call-done = f32[96,192]{1,0:T(8,128)} async-done(((f32[768,192]{1,0:T(8,128)}), f32[96,192]{1,0:T(8,128)}) %reduce-scatter.15.cloned.1.call-update) | async-done | bytes 73744 | tf_op jit(solution)/shard_map/reduce_scatter | solution.py:310
  (185 shorter events, 149.5 us)
Async XLA Ops:
  7.2 107.7 %copy-start.1 = (bf16[1,750,768]{2,1,0:T(8,128)(2,1)S(1)}, bf16[1,750,768]{2,1,0:T(8,128)(2,1)}, u32[]{:S(2)}) copy-start(bf16[1,750,768]{2,1,0:T(8,128)(2,1)} %param.17) | copy-start | bytes 3456004
  7.2 37.5 %copy-start.29 = (bf16[192,96]{1,0:T(8,128)(2,1)S(1)}, bf16[192,96]{1,0:T(8,128)(2,1)}, u32[]{:S(2)}) copy-start(bf16[192,96]{1,0:T(8,128)(2,1)} %param.25) | copy-start | bytes 110596
  7.2 53.5 %copy-start.26 = (bf16[96,192]{1,0:T(8,128)(2,1)S(1)}, bf16[96,192]{1,0:T(8,128)(2,1)}, u32[]{:S(2)}) copy-start(bf16[96,192]{1,0:T(8,128)(2,1)} %param.20) | copy-start | bytes 110596
  7.2 72.6 %copy-start.27 = (bf16[96,192]{1,0:T(8,128)(2,1)S(1)}, bf16[96,192]{1,0:T(8,128)(2,1)}, u32[]{:S(2)}) copy-start(bf16[96,192]{1,0:T(8,128)(2,1)} %param.22) | copy-start | bytes 110596
  7.2 88.5 %copy-start.28 = (bf16[96,192]{1,0:T(8,128)(2,1)S(1)}, bf16[96,192]{1,0:T(8,128)(2,1)}, u32[]{:S(2)}) copy-start(bf16[96,192]{1,0:T(8,128)(2,1)} %param.23) | copy-start | bytes 110596
  7.2 327.0 %all-gather.23.cloned.1.call-start = ((), (), s32[]{:S(2)}) async-start(), calls=%async_computation.13 | async-start | bytes 11550720 | tf_op jit(solution)/shard_map/all_gather | solution.py:61
  60.7 107.0 %copy-start.11 = (bf16[192,768]{0,1:T(8,128)(2,1)}, bf16[192,768]{0,1:T(8,128)(2,1)S(1)}, u32[]{:S(2)}) copy-start(bf16[192,768]{0,1:T(8,128)(2,1)S(1)} %all_gather.81) | copy-start | bytes 884740
  95.7 30.2 %copy-start.10 = (bf16[768,192]{1,0:T(8,128)(2,1)}, bf16[768,192]{1,0:T(8,128)(2,1)S(1)}, u32[]{:S(2)}) copy-start(bf16[768,192]{1,0:T(8,128)(2,1)S(1)} %all_gather.79) | copy-start | bytes 884740
  129.6 17.1 %copy-start.6 = (bf16[1500,3,64]{0,2,1:T(8,128)(2,1)}, bf16[1500,3,64]{0,2,1:T(8,128)(2,1)S(1)}, u32[]{:S(2)}) copy-start(bf16[1500,3,64]{0,2,1:T(8,128)(2,1)S(1)} %reshape.472) | copy-start | bytes 1728004
  170.3 187.9 %all-gather.19.cloned.1.call-start = ((), (), s32[]{:S(2)}) async-start(), calls=%async_computation.6 | async-start | bytes 1327104 | tf_op jit(solution)/shard_map/all_gather | solution.py:50
  171.0 213.0 %all-gather.21.cloned.1.call-start = ((), (), s32[]{:S(2)}) async-start(), calls=%async_computation.7 | async-start | bytes 1327104 | tf_op jit(solution)/shard_map/all_gather | solution.py:55
  171.8 384.2 %all-gather.27.cloned.1.call-start = ((), (), s32[]{:S(2)}) async-start(), calls=%async_computation.15 | async-start | bytes 11550720 | tf_op jit(solution)/shard_map/all_gather | solution.py:61
  392.3 326.9 %all-gather.25.cloned.1.call-start = ((), (), s32[]{:S(2)}) async-start(), calls=%async_computation.14 | async-start | bytes 11550720 | tf_op jit(solution)/shard_map/all_gather | solution.py:61
  396.5 485.9 %all-gather.29.cloned.1.call-start = ((), (), s32[]{:S(2)}) async-start(), calls=%async_computation.16 | async-start | bytes 11550720 | tf_op jit(solution)/shard_map/all_gather | solution.py:61
  561.1 12.9 %slice-start = ((s8[13860864]{0:T(1024)(128)(4,1)}), s8[4194304]{0:T(1024)(128)(4,1)S(1)}, s32[]{:S(2)}) async-start(s8[13860864]{0:T(1024)(128)(4,1)} %bitcast.162), calls=%async_computation.18 | async-start | bytes 8388608
  562.4 11.5 %slice-start.1 = ((s8[13860864]{0:T(1024)(128)(4,1)}), s8[4194304]{0:T(1024)(128)(4,1)S(1)}, s32[]{:S(2)}) async-start(s8[13860864]{0:T(1024)(128)(4,1)} %bitcast.162), calls=%async_computation.19 | async-start | bytes 8388608
  565.2 8.8 slice-start.2
  663.0 255.7 %reduce-scatter.21.cloned.1.call-start = ((), (), s32[]{:S(2)}) async-start(), calls=%async_computation.17 | async-start | bytes 884736
  734.6 230.3 %reduce-scatter.17.cloned.1.call-start = ((), (), s32[]{:S(2)}) async-start(), calls=%async_computation.11 | async-start | bytes 2654208 | tf_op jit(solution)/shard_map/reduce_scatter | solution.py:314
  738.9 272.4 %reduce-scatter.19.cloned.1.call-start = ((), (), s32[]{:S(2)}) async-start(), calls=%async_computation.12 | async-start | bytes 2654208 | tf_op jit(solution)/shard_map/reduce_scatter | solution.py:319
  743.0 306.8 %reduce-scatter.13.cloned.1.call-start = ((), (), s32[]{:S(2)}) async-start(), calls=%async_computation.9 | async-start | bytes 884736 | tf_op jit(solution)/shard_map/reduce_scatter | solution.py:309
  889.1 10.0 copy-start.25
  900.7 187.8 %reduce-scatter.11.cloned.1.call-start = ((), (), s32[]{:S(2)}) async-start(), calls=%async_computation.8 | async-start | bytes 884736 | tf_op jit(solution)/shard_map/reduce_scatter | solution.py:308
  902.2 224.8 %reduce-scatter.15.cloned.1.call-start = ((), (), s32[]{:S(2)}) async-start(), calls=%async_computation.10 | async-start | bytes 884736 | tf_op jit(solution)/shard_map/reduce_scatter | solution.py:310
  (27 other events, 106.1 us)
Sparse Core Ops, SparseCore 0:
  170.4 163.7 all-gather.22
  336.1 22.0 all-gather.18
  360.1 23.9 all-gather.20
  392.4 163.5 all-gather.26
  557.4 161.7 all-gather.24
  720.6 161.7 all-gather.28
  885.5 33.0 reduce-scatter.20
  922.6 42.3 reduce-scatter.16
  968.9 42.3 reduce-scatter.18
  1014.9 34.9 reduce-scatter.12
  1053.5 34.9 reduce-scatter.10
  1092.1 34.9 reduce-scatter.14
